TPU v7x, 32 devices: a whole 2x2x4 slice. The times are simulated.
32 devices in a mesh: seq: 4 (over z), wt: 8 (over y, x, core).
Axes of the slice: x: 2, y: 2, z: 4, core: 2. Of those that a mesh axis runs over, the one named last changes fastest.
Arguments:
- tokens: bfloat16 [8, 512, 2048], P('wt', 'seq'), may hold values from -6 to 6
- cotangent: bfloat16 [8, 512, 2048], P('wt', 'seq'), may hold values from -6 to 6
- segment_ids: int32 [8, 512], P('wt'), may hold values from 0 to 1, never falling along the last dimension, each value on 1 to 320 neighbouring positions
- expert_routes: int32 [8, 512, 8], P('wt', 'seq'), may hold values from 0 to 15, all different within a row; in each aligned block of 128 rows (0 to 127, 128 to 255, ..., all dimensions but the last counted through in order) at most 128 rows name the same one
- w_qkv: bfloat16 [2048, 6144], P('wt'), may hold values from -0.125 to 0.125
- w_out: bfloat16 [2048, 2048], P('wt'), may hold values from -2 to 2
- w_router: bfloat16 [2048, 16], P('wt'), may hold values from -0.0625 to 0.0625
- w_gate_up: bfloat16 [16, 2048, 2048], P('seq', 'wt'), may hold values from -0.125 to 0.125
- w_down: bfloat16 [16, 1024, 2048], P('seq', 'wt'), may hold values from -0.75 to 0.75
- attn_gain: bfloat16 [2048], P('wt'), may hold values from 0.5 to 1.5
- ffn_gain: bfloat16 [2048], P('wt'), may hold values from 0.5 to 1.5
- q_gain: bfloat16 [128], P('wt'), may hold values from 0.5 to 1.5
- k_gain: bfloat16 [128], P('wt'), may hold values from 0.5 to 1.5
Outputs:
- output: bfloat16 [8, 512, 2048], P('wt', 'seq')
- tokens_grad: float32 [8, 512, 2048], P('wt', 'seq')
- w_qkv_grad: float32 [2048, 6144], P('wt')
- w_out_grad: float32 [2048, 2048], P('wt')
- w_router_grad: float32 [2048, 16], P('wt')
- w_gate_up_grad: float32 [16, 2048, 2048], P('seq', 'wt')
- w_down_grad: float32 [16, 1024, 2048], P('seq', 'wt')
- attn_gain_grad: float32 [2048], P('wt')
- ffn_gain_grad: float32 [2048], P('wt')
- q_gain_grad: float32 [128], P('wt')
- k_gain_grad: float32 [128], P('wt')
Inputs may be any that keep to these rules, and one draw needn't show every extreme that they name: `segment_ids`: along a sequence the segment numbers never fall; each of the 2 documents spans 1 to 320 positions. `expert_routes`: A token names 8 different experts; among the 128 tokens of one device no expert is named more than 128 times, a bound that some block reaches.
All inputs are finite; a program needn't handle non-finite values.
Results may differ from a plain program's by a relative error of at most 0.028.
Values may be sent and summed in bfloat16 or wider, within the bound.
A program may use at most 512 MiB of HBM per device.

v0:
```python
import jax
import jax.numpy as jnp
import numpy as np
from jax import lax
from jax.sharding import PartitionSpec as P


H = 16
HD = 128
FF = 1024

EPS = 1e-06
THETA = 50000.0
NEG = -1e30
LANES = 128
BF = jnp.bfloat16
F32 = jnp.float32


def normalize(values):
    factor = lax.rsqrt(jnp.mean(values * values, axis=-1, keepdims=True) + EPS)
    return (values * factor, factor)


def norm_back(grad_normed, normed_values, factor):
    return factor * (
        grad_normed - normed_values * jnp.mean(grad_normed * normed_values, axis=-1, keepdims=True)
    )


def rope_tables(length):
    half = HD // 2
    freq = THETA ** (-jnp.arange(half, dtype=F32) * 2.0 / HD)
    angle = jnp.arange(length, dtype=F32)[:, None] * freq[None, :]
    return jnp.cos(angle)[:, None, :], jnp.sin(angle)[:, None, :]


def rotate(values, cosine, sine):
    half = values.shape[-1] // 2
    first = values[..., :half]
    second = values[..., half:]
    return jnp.concatenate(
        [first * cosine - second * sine, second * cosine + first * sine], axis=-1
    )


def dot(left, right, dims):
    return lax.dot_general(left, right, (dims, ((), ())), preferred_element_type=F32)


def nn(left, right):
    return dot(left, right, ((1,), (0,)))


def nt(left, right):
    return dot(left, right, ((1,), (1,)))


def tn(left, right):
    return dot(left, right, ((0,), (0,)))


def split_two(values):
    high = values.astype(BF)
    low = (values - high.astype(F32)).astype(BF)
    return high, low


def swap(values, bit):
    total = lax.axis_size("wt")
    return lax.ppermute(values, "wt", [(i, i ^ bit) for i in range(total)])


def bits_of(chips, route):
    bits = []
    while 1 << len(bits) < chips:
        bits.append(1 << len(bits))
    return bits[::-1] if route else bits


def zero_of(anchor):
    return anchor[(0,) * anchor.ndim].astype(F32) * 0.0


def later(values, anchor):
    return (values.astype(F32) + zero_of(anchor)).astype(values.dtype)


def first_gather(own, route, chips):
    bits = bits_of(chips, route)
    return {bit: swap(own, 2 * bit) for bit in bits}


def rest_gather(own, direct, route, chips, anchor, use):
    pieces = {0: own}
    handed = {0}
    for bit in bits_of(chips, route):
        for mask in list(pieces):
            if mask:
                if mask not in handed:
                    pieces[mask] = later(pieces[mask], anchor)
                    handed.add(mask)
                pieces[mask ^ bit] = swap(pieces[mask], 2 * bit)
            else:
                pieces[bit] = direct[bit]
    return [
        pieces[mask] if mask in handed else later(pieces[mask], use) for mask in range(chips)
    ]


def gather_chips(own, route, chips):
    bits = bits_of(chips, route)
    pieces = {0: own}
    for bit in bits:
        for mask in list(pieces):
            pieces[mask ^ bit] = swap(pieces[mask], 2 * bit)
    return [pieces[mask] for mask in range(chips)]


def send_first(parts, route, chips):
    bit = bits_of(chips, route)[0]
    return {mask: swap(parts[mask], 2 * bit) for mask in range(chips) if mask & bit}


def scatter_chips(parts, route, chips, first=None, anchor=None):
    bits = bits_of(chips, route)
    held = dict(enumerate(parts))
    if first is None:
        first = send_first(parts, route, chips)
    zero = 0.0 if anchor is None else zero_of(anchor)
    for place, bit in enumerate(bits):
        for mask in [m for m in held if m & bit]:
            sent = held.pop(mask)
            arrived = swap(sent, 2 * bit) if place else first[mask]
            total = held[mask ^ bit].astype(F32) + arrived.astype(F32) + zero
            rest = [b for b in bits[place + 1 :] if (mask ^ bit) & b]
            held[mask ^ bit] = total.astype(BF) if rest else total
    return held[0]


def body(
    tokens,
    cotangent,
    segment_ids,
    expert_routes,
    w_qkv,
    w_out,
    w_router,
    w_gate_up,
    w_down,
    attn_gain,
    ffn_gain,
    q_gain,
    k_gain,
):
    seq_total = lax.axis_size("seq")
    wt_total = lax.axis_size("wt")
    seq_me = lax.axis_index("seq")
    wt_me = lax.axis_index("wt")
    core = wt_me % 2
    chip = wt_me // 2
    chips = wt_total // 2
    first_core = core == 0
    rows = tokens.shape[1]
    model = tokens.shape[2]
    length = rows * seq_total
    shard = model // wt_total
    local_experts = w_gate_up.shape[0]
    experts = w_router.shape[1]
    heads = H // seq_total
    part = heads * HD
    cols = 3 * part
    gain_part = q_gain.shape[0]
    half = model // 2
    order = [2 * m for m in range(chips)] + [2 * m + 1 for m in range(chips)]
    slim = FF // wt_total

    def pick_blocks(values, places, width):
        return jnp.concatenate(
            [lax.dynamic_slice_in_dim(values, place * width, width, axis=1) for place in places],
            axis=1,
        )

    def to_relative(values):
        return pick_blocks(values, [wt_me ^ mask for mask in order], shard)

    def from_relative(values):
        masks = [wt_me ^ device for device in range(wt_total)]
        return pick_blocks(values, [mask // 2 + (mask % 2) * chips for mask in masks], shard)

    def by_chip(values):
        return pick_blocks(values, [chip ^ mask for mask in range(chips)], 2 * shard)

    small = jnp.concatenate(
        [
            w_router,
            attn_gain[:, None],
            ffn_gain[:, None],
            jnp.pad(q_gain, (0, shard - gain_part))[:, None],
            jnp.pad(k_gain, (0, shard - gain_part))[:, None],
        ],
        axis=1,
    )
    small = jnp.pad(small, ((0, 0), (0, LANES - small.shape[1])))
    qkv_here = jnp.concatenate(
        [
            lax.dynamic_slice_in_dim(w_qkv, kind * H * HD + seq_me * part, part, axis=1)
            for kind in range(3)
        ]
        + [small],
        axis=1,
    )
    token_ids = jnp.arange(experts, dtype=jnp.int32)
    routed_own = jnp.any(expert_routes[0][:, :, None] == token_ids[None, None, :], axis=1)
    tokens_sent = jnp.concatenate(
        [
            to_relative(tokens[0]),
            jnp.pad(routed_own.astype(BF), ((0, 0), (0, LANES - experts))),
        ],
        axis=1,
    )
    tokens_got = lax.all_gather(tokens_sent, "seq", axis=0, tiled=True)
    tokens_all = tokens_got[:, :model]
    routed = tokens_got[:, model : model + experts] > 0.5

    qkv_pieces = gather_chips(qkv_here, 0, chips)
    out_pieces = gather_chips(w_out, 1, chips)
    qkv_blocks = qkv_pieces + [swap(piece, 1) for piece in qkv_pieces]
    out_even = jnp.concatenate(out_pieces, axis=0)
    out_odd = swap(out_even, 1)

    def columns_of(values, which):
        return jnp.concatenate(
            [
                values[:, (2 * j + which) * slim : (2 * j + which + 1) * slim]
                for j in range(wt_total)
            ],
            axis=1,
        )

    pairs = []
    pairs_direct = []
    downs_own = []
    downs_direct = []

    def send_expert(e, anchor):
        zero = zero_of(anchor)
        low_half = columns_of(w_gate_up[e], 0)
        high_half = columns_of(w_gate_up[e], 1)
        mine = jnp.where(first_core, low_half, high_half)
        others = swap(jnp.where(first_core, high_half, low_half), 1)
        pair = jnp.where(
            first_core,
            jnp.concatenate([mine, others], axis=0),
            jnp.concatenate([others, mine], axis=0),
        )
        pair = (pair.astype(F32) + zero).astype(BF)
        down_own = (w_down[e].astype(F32) + zero).astype(BF)
        pairs.append(pair)
        downs_own.append(down_own)
        pairs_direct.append(first_gather(pair, e % 2, chips))
        downs_direct.append(first_gather(down_own, 1 - e % 2, chips))

    def expert_weights(e, anchor, use):
        pieces = rest_gather(pairs[e], pairs_direct[e], e % 2, chips, anchor, use)
        down_pieces = rest_gather(
            downs_own[e], downs_direct[e], 1 - e % 2, chips, anchor, use
        )
        down = jnp.zeros((FF // 2, model), BF)
        for mask in range(chips):
            down = lax.dynamic_update_slice_in_dim(
                down, down_pieces[mask], (chip ^ mask) * slim, axis=0
            )
        return jnp.concatenate(pieces, axis=0), down

    starts = [qkv_pieces[-1], qkv_pieces[-1], out_pieces[1]]
    for e in range(min(local_experts, 3)):
        send_expert(e, starts[e])

    grad_own = later(cotangent[0], tokens_got)
    grad_seq = lax.all_gather(grad_own, "seq", axis=0, tiled=True)
    grad_two = jnp.concatenate([grad_seq, swap(grad_seq, 1)], axis=0)

    small_relative = jnp.concatenate([block[:, cols:] for block in qkv_blocks], axis=0)
    router = jnp.concatenate(
        [
            lax.dynamic_slice_in_dim(
                small_relative, (mask + (side ^ core) * chips) * shard, shard, axis=0
            )
            for mask in range(chips)
            for side in range(2)
        ],
        axis=0,
    )[:, :experts]
    picker = np.zeros((8, LANES), np.float32)
    for row in range(4):
        picker[row, experts + row] = 1.0
    gain_rows = nt(jnp.asarray(picker, BF), small_relative)
    gain_attn_relative = gain_rows[0]
    gain_rows = from_relative(gain_rows)
    gain_attn = gain_rows[0]
    gain_ffn = gain_rows[1]
    gain_query = gain_rows[2].reshape(wt_total, shard)[:, :gain_part].reshape(HD)
    gain_key = gain_rows[3].reshape(wt_total, shard)[:, :gain_part].reshape(HD)

    segments = segment_ids[0]
    same = segments[:, None] == segments[None, :]
    cosine, sine = rope_tables(length)
    normed_all, _ = normalize(tokens_all.astype(F32))
    hidden = (normed_all * gain_attn_relative).astype(BF)
    qkv_full = jnp.zeros((model, cols), BF)
    for place, block in enumerate(qkv_blocks):
        qkv_full = lax.dynamic_update_slice_in_dim(
            qkv_full, block[:, :cols], place * shard, axis=0
        )
    projected = nn(hidden, qkv_full)
    projected = projected.reshape(length, 3, heads, HD)
    normed_q, factor_q = normalize(projected[:, 0])
    normed_k, factor_k = normalize(projected[:, 1])
    queries = jnp.swapaxes(rotate(normed_q * gain_query, cosine, sine).astype(BF), 0, 1)
    keys = jnp.swapaxes(rotate(normed_k * gain_key, cosine, sine).astype(BF), 0, 1)
    values = jnp.swapaxes(projected[:, 2].astype(BF), 0, 1)
    scale = HD ** (-0.5)

    def bmm(left, right, dims):
        return lax.dot_general(left, right, (dims, ((0,), (0,))), preferred_element_type=F32)

    logits = jnp.where(same[None], bmm(queries, keys, ((2,), (2,))) * scale, NEG)
    powers = jnp.exp(logits - jnp.max(logits, axis=-1, keepdims=True))
    weights = powers / jnp.sum(powers, axis=-1, keepdims=True)
    weights_low = weights.astype(BF)
    attended = bmm(weights_low, values, ((2,), (1,))).astype(BF)
    merged = lax.all_to_all(
        jnp.swapaxes(attended, 0, 1), "seq", split_axis=0, concat_axis=1, tiled=True
    ).reshape(rows, H * HD)
    for e in range(min(local_experts, 3), local_experts):
        send_expert(e, attended)
    merged = to_relative(merged)

    inputs = tokens[0].astype(F32)
    residual = inputs + nn(merged[:, :half], out_even) + nn(merged[:, half:], out_odd)
    normed_f, factor_f = normalize(residual)
    hidden_own = (normed_f * gain_ffn).astype(BF)
    hidden_sent = by_chip(hidden_own)
    hidden_seq = lax.all_gather(hidden_sent, "seq", axis=0, tiled=True)
    forward_marks = [attended, merged, hidden_own]
    use_marks = [hidden_own, hidden_own]
    gate_ups = []
    downs = []
    for e in range(min(local_experts, 2)):
        gate_up, down = expert_weights(e, forward_marks[e], use_marks[e])
        gate_ups.append(gate_up)
        downs.append(down)
    hidden_two = jnp.concatenate([hidden_seq, swap(hidden_seq, 1)], axis=0)

    chances = jax.nn.softmax(nn(hidden_seq, router), axis=-1)
    picked = jnp.where(routed, chances, 0.0)
    picked_total = jnp.sum(picked, axis=1, keepdims=True)
    gates = picked / picked_total
    gates_seq = lax.dynamic_slice_in_dim(gates, seq_me * local_experts, local_experts, axis=1)
    gates_two = jnp.concatenate([gates_seq, swap(gates_seq, 1)], axis=0)

    grad_hidden_part = jnp.zeros((2 * length, model), F32)
    gate_grads = []
    wide_grads = []
    scaled_all = []
    for e in range(local_experts):
        gate = gates_two[:, e : e + 1]
        if e >= 2:
            mark = hidden_seq if e == 2 else wide_grads[e - 3]
            gate_up, down = expert_weights(e, mark, wide_grads[e - 2])
            gate_ups.append(gate_up)
            downs.append(down)
        before = nn(hidden_two, gate_ups[e])
        gate_part = before[:, : FF // 2]
        up_part = before[:, FF // 2 :]
        sigmoid_gate = jax.nn.sigmoid(gate_part)
        silu_gate = gate_part * sigmoid_gate
        activated = silu_gate * up_part
        scaled = (gate * activated).astype(BF)
        grad_act = nt(grad_two, downs[e])
        gate_grads.append(jnp.sum(grad_act * activated, axis=1, keepdims=True))
        grad_act = grad_act * gate
        grad_gate = grad_act * up_part * sigmoid_gate * (1.0 + gate_part * (1.0 - sigmoid_gate))
        grad_up = grad_act * silu_gate
        grad_before = jnp.concatenate([grad_gate, grad_up], axis=-1).astype(BF)
        grad_hidden_part = grad_hidden_part + nt(grad_before, gate_ups[e])
        wide_grads.append(grad_before)
        scaled_all.append(scaled)

    gate_grad_two = jnp.concatenate(gate_grads, axis=1)
    gate_grad_part = gate_grad_two[:length] + swap(gate_grad_two[length:], 1)
    gate_high, gate_low = split_two(gate_grad_part)
    grad_hidden_low = (
        grad_hidden_part[:length] + swap(grad_hidden_part[length:].astype(BF), 1).astype(F32)
    ).astype(BF)

    def spread(values):
        wide = jnp.zeros((length, experts), BF)
        return lax.dynamic_update_slice(wide, values, (0, seq_me * local_experts))

    payload = jnp.concatenate([grad_hidden_low, spread(gate_high), spread(gate_low)], axis=1)
    returned = lax.psum_scatter(payload, "seq", scatter_dimension=0, tiled=True)
    returned = returned.astype(F32)
    gate_grad = returned[:, model : model + experts] + returned[:, model + experts :]
    expert_parts = []

    def start_expert(e, anchor):
        wide = later(wide_grads[e], anchor)
        scaled = later(scaled_all[e], anchor)
        parts = [
            tn(hidden_two[:, mask * 2 * shard : (mask + 1) * 2 * shard], wide).astype(BF)
            for mask in range(chips)
        ]
        down_grad = tn(scaled, grad_two).astype(BF)
        down_parts = [
            lax.dynamic_slice_in_dim(down_grad, (chip ^ mask) * slim, slim, axis=0)
            for mask in range(chips)
        ]
        sent = send_first(parts, e % 2, chips)
        down_sent = send_first(down_parts, 1 - e % 2, chips)
        expert_parts.append((parts, sent, down_parts, down_sent))

    start_expert(0, payload)
    start_expert(1, payload)

    def finish_expert(e, anchor):
        parts, first, down_parts, down_first = expert_parts[e]
        summed = scatter_chips(parts, e % 2, chips, first, anchor).astype(BF)
        down_row = scatter_chips(down_parts, 1 - e % 2, chips, down_first, anchor)
        kept = lax.dynamic_slice_in_dim(summed, core * shard, shard, axis=0)
        sent = lax.dynamic_slice_in_dim(summed, (1 - core) * shard, shard, axis=0)
        got = swap(sent, 1)
        low_half = jnp.where(first_core, kept, got)
        high_half = jnp.where(first_core, got, kept)
        gate_up_row = jnp.concatenate(
            [
                source[:, j * slim : (j + 1) * slim]
                for j in range(wt_total)
                for source in (low_half, high_half)
            ],
            axis=1,
        ).astype(F32)
        return gate_up_row, down_row

    def own(full):
        return lax.dynamic_slice_in_dim(full, seq_me * rows, rows, axis=0)

    chances_own = own(chances)
    gates_own = own(gates)
    inner_gate = jnp.sum(gate_grad * gates_own, axis=1, keepdims=True)
    grad_chances = jnp.where(routed_own, (gate_grad - inner_gate) / own(picked_total), 0.0)
    grad_logits = (
        chances_own
        * (grad_chances - jnp.sum(grad_chances * chances_own, axis=1, keepdims=True))
    ).astype(BF)
    grad_hidden = by_chip(returned[:, :model] + nt(grad_logits, router))
    router_grad = tn(
        to_relative(hidden_own), jnp.pad(grad_logits, ((0, 0), (0, LANES - experts)))
    )
    ffn_gain_grad = jnp.sum(grad_hidden * normed_f, axis=0)
    grad_residual = cotangent[0].astype(F32) + norm_back(
        grad_hidden * gain_ffn, normed_f, factor_f
    )
    grad_branch = grad_residual.astype(BF)
    grad_merged = jnp.concatenate(
        [nt(grad_branch, out_even), nt(grad_branch, out_odd)], axis=1
    )
    grad_merged = from_relative(grad_merged.astype(BF))
    for e in range(2, min(local_experts, 3)):
        start_expert(e, grad_merged)
    grad_merged = grad_merged.reshape(rows, H, HD)
    grad_heads = jnp.swapaxes(
        lax.all_to_all(grad_merged, "seq", split_axis=1, concat_axis=0, tiled=True), 0, 1
    )

    scaled_out = [later(scaled, grad_heads) for scaled in scaled_all]
    out_part = jnp.zeros((2 * length, model), F32)
    for e in range(local_experts):
        out_part = out_part + nn(scaled_out[e], downs[e])
    out_other = swap(out_part[length:].astype(BF), 1)
    out_low = (out_part[:length] + out_other.astype(F32)).astype(BF)
    moe_out = lax.psum_scatter(out_low, "seq", scatter_dimension=0, tiled=True)
    moe_out = moe_out.astype(F32)

    def scatter_rows(left, right, route):
        sent = tn(left[:, half:], right).astype(BF)
        other = swap(sent, 1)
        kept = (tn(left[:, :half], right) + other.astype(F32)).astype(BF)
        parts = [kept[mask * shard : (mask + 1) * shard] for mask in range(chips)]
        first = send_first(parts, route, chips)
        return scatter_chips(parts, route, chips, first).astype(BF)

    out_sum = scatter_rows(later(merged, grad_merged), grad_branch, 1)

    out_grad = lax.psum(out_sum, "seq")
    out_grad = out_grad.astype(F32)

    grad_v = jnp.swapaxes(bmm(weights_low, grad_heads, ((1,), (1,))), 0, 1)
    grad_weights = bmm(grad_heads, values, ((2,), (2,)))
    inner = jnp.sum(weights * grad_weights, axis=-1, keepdims=True)
    grad_scores = (weights * (grad_weights - inner)).astype(BF)
    grad_q = jnp.swapaxes(bmm(grad_scores, keys, ((2,), (1,))), 0, 1) * scale
    grad_k = jnp.swapaxes(bmm(grad_scores, queries, ((1,), (1,))), 0, 1) * scale
    grad_q_normed = rotate(grad_q, cosine, -sine)
    grad_k_normed = rotate(grad_k, cosine, -sine)
    q_gain_grad = jnp.sum(grad_q_normed * normed_q, axis=(0, 1))
    k_gain_grad = jnp.sum(grad_k_normed * normed_k, axis=(0, 1))
    grad_q_raw = norm_back(grad_q_normed * gain_query, normed_q, factor_q)
    grad_k_raw = norm_back(grad_k_normed * gain_key, normed_k, factor_k)
    grads = [g.reshape(length, part).astype(BF) for g in (grad_q_raw, grad_k_raw, grad_v)]
    grad_projected = jnp.concatenate(grads, axis=1)
    grad_normed_part = nt(grad_projected, qkv_full)
    attn_gain_grad = jnp.sum(grad_normed_part * normed_all, axis=0)
    grad_normed_low = grad_normed_part.astype(BF)
    grad_normed_own = lax.psum_scatter(
        grad_normed_low, "seq", scatter_dimension=0, tiled=True
    )
    grad_normed_own = grad_normed_own.astype(F32)
    grad_normed_own = from_relative(grad_normed_own)
    normed_a, factor_a = normalize(inputs)
    tokens_grad = grad_residual + norm_back(grad_normed_own * gain_attn, normed_a, factor_a)

    def gain_line(vector):
        return jnp.pad(
            vector.reshape(wt_total, gain_part), ((0, 0), (0, shard - gain_part))
        ).reshape(model)

    lines = to_relative(
        jnp.stack([ffn_gain_grad, gain_line(q_gain_grad), gain_line(k_gain_grad)])
    )
    lines = jnp.concatenate([attn_gain_grad[None], lines, jnp.zeros((4, model), F32)], axis=0)
    small_grad = router_grad + tn(lines.astype(BF), jnp.asarray(picker, BF))
    small_sent = small_grad[half:].astype(BF)
    small_kept = (small_grad[:half] + swap(small_sent, 1).astype(F32)).astype(BF)
    small_sum = scatter_chips(
        [small_kept[mask * shard : (mask + 1) * shard] for mask in range(chips)], 1, chips
    ).astype(BF)
    for e in range(3, local_experts):
        start_expert(e, grad_normed_low)
    value_sum = scatter_rows(hidden, grads[2], 0)
    query_sum = scatter_rows(hidden, grads[0], 1)
    key_sum = scatter_rows(hidden, grads[1], 0)
    collected_value = lax.all_gather(value_sum, "seq", axis=0)
    collected = lax.all_gather(
        jnp.concatenate([query_sum, key_sum, small_sum], axis=1), "seq", axis=0
    )
    qkv_out = jnp.concatenate(
        [collected[z, :, :part] for z in range(seq_total)]
        + [collected[z, :, part : 2 * part] for z in range(seq_total)]
        + [collected_value[z] for z in range(seq_total)],
        axis=1,
    ).astype(F32)
    small_out = jnp.sum(collected[:, :, 2 * part :].astype(F32), axis=0)
    anchors = [grad_heads, grad_projected, query_sum, key_sum]
    expert_rows = [
        finish_expert(e, anchors[min(e * len(anchors) // local_experts, len(anchors) - 1)])
        for e in range(local_experts)
    ]
    gate_up_out = jnp.stack([row[0] for row in expert_rows])
    down_out = jnp.stack([row[1] for row in expert_rows])
    output = (residual + moe_out + zero_of(grad_projected)).astype(BF)
    return (
        output[None],
        tokens_grad[None],
        qkv_out,
        out_grad,
        small_out[:, :experts],
        gate_up_out,
        down_out,
        small_out[:, experts],
        small_out[:, experts + 1],
        small_out[:gain_part, experts + 2],
        small_out[:gain_part, experts + 3],
    )


def solution(mesh):
    in_specs = (
        P("wt", "seq", None),
        P("wt", "seq", None),
        P("wt", None),
        P("wt", "seq", None),
        P("wt", None),
        P("wt", None),
        P("wt", None),
        P("seq", "wt", None),
        P("seq", "wt", None),
        P("wt"),
        P("wt"),
        P("wt"),
        P("wt"),
    )
    out_specs = (
        P("wt", "seq", None),
        P("wt", "seq", None),
        P("wt", None),
        P("wt", None),
        P("wt", None),
        P("seq", "wt", None),
        P("seq", "wt", None),
        P("wt"),
        P("wt"),
        P("wt"),
        P("wt"),
    )

    return jax.shard_map(body, mesh=mesh, in_specs=in_specs, out_specs=out_specs, check_vma=False)
```

profile of v0, /device:TPU:0, one launch (start us, length us, event | category | flops | bytes accessed | tf_op | source)
XLA Modules:
  0.0 1073.7 jit_solution(8388626624116394423)
XLA Ops:
  87.4 9.5 collective-permute-done.2
  116.8 15.2 %collective-permute-done.9 = bf16[256,2048]{1,0:T(8,128)(2,1)S(1)} collective-permute-done((bf16[256,2048]{1,0:T(8,128)(2,1)}, bf16[256,2048]{1,0:T(8,128)(2,1)S(1)}, u32[]{:S(2)}, u32[]{:S(2)}) %collective-permute-start.9) | collective-permute-done | bytes 1048608 | tf_op jit(solution)/shard_map/ppermute | solution.py:71
  197.1 14.7 %collective-permute-done.26 = bf16[512,1024]{1,0:T(8,128)(2,1)} collective-permute-done((bf16[512,1024]{1,0:T(8,128)(2,1)}, bf16[512,1024]{1,0:T(8,128)(2,1)}, u32[]{:S(2)}, u32[]{:S(2)}) %collective-permute-start.26) | collective-permute-done | bytes 1048608 | tf_op jit(solution)/shard_map/ppermute | solution.py:71
  229.8 20.1 %collective-permute-done.18 = bf16[128,2048]{1,0:T(8,128)(2,1)} collective-permute-done((bf16[128,2048]{1,0:T(8,128)(2,1)}, bf16[128,2048]{1,0:T(8,128)(2,1)}, u32[]{:S(2)}, u32[]{:S(2)}) %collective-permute-start.18) | collective-permute-done | bytes 524320 | tf_op jit(solution)/shard_map/ppermute | solution.py:71
  258.7 17.4 %collective-permute-done.16 = bf16[512,1024]{1,0:T(8,128)(2,1)S(1)} collective-permute-done((bf16[512,1024]{1,0:T(8,128)(2,1)}, bf16[512,1024]{1,0:T(8,128)(2,1)S(1)}, u32[]{:S(2)}, u32[]{:S(2)}) %collective-permute-start.16) | collective-permute-done | bytes 1048608 | tf_op jit(solution)/shard_map/ppermute | solution.py:71
  281.3 13.6 %collective-permute-done.23 = bf16[128,2048]{1,0:T(8,128)(2,1)} collective-permute-done((bf16[128,2048]{1,0:T(8,128)(2,1)}, bf16[128,2048]{1,0:T(8,128)(2,1)}, u32[]{:S(2)}, u32[]{:S(2)}) %collective-permute-start.23) | collective-permute-done | bytes 524320 | tf_op jit(solution)/shard_map/ppermute | solution.py:71
  306.1 32.8 %collective-permute-done.20 = bf16[128,2048]{1,0:T(8,128)(2,1)} collective-permute-done((bf16[128,2048]{1,0:T(8,128)(2,1)S(1)}, bf16[128,2048]{1,0:T(8,128)(2,1)}, u32[]{:S(2)}, u32[]{:S(2)}) %collective-permute-start.20) | collective-permute-done | bytes 524320 | tf_op jit(solution)/shard_map/ppermute | solution.py:71
  402.8 9.7 fusion.41
  435.3 10.0 fusion.40
  454.4 10.0 fusion.39
  474.4 18.1 %add_add_fusion.1 = f32[1024,2048]{1,0:T(8,128)} fusion(f32[1024,2048]{1,0:T(8,128)} %fusion.39, f32[1024,2048]{1,0:T(8,128)} %fusion.41, f32[1024,2048]{1,0:T(8,128)} %fusion.40, bf16[1024,512]{1,0:T(8,128)(2,1)} %get-tuple-element.112, bf16[1024,512]{1,0:T(8,128)(2,1)} %get-tuple-element.111, bf16[512,1024]{1,0:T(8,128)(2,1)} %copy-done.26, ...), kind=kOutput, calls=%fused_computation.7 | convolution fusion | flops 4322230272 | bytes 39845888 | tf_op jit(solution)/shard_map/dot_general | solution.py:48
  558.5 12.0 %reduce-scatter.4.cloned.1.call-done = bf16[128,2080]{1,0:T(8,128)(2,1)} async-done(((bf16[512,2080]{1,0:T(8,128)(2,1)}), bf16[128,2080]{1,0:T(8,128)(2,1)}) %reduce-scatter.4.cloned.1.call-update) | async-done | bytes 532496 | tf_op jit(solution)/shard_map/reduce_scatter | solution.py:403
  699.9 11.0 %add_add_fusion = f32[1024,2048]{1,0:T(8,128)S(1)} fusion(f32[1024,2048]{1,0:T(8,128)} %fusion.54, f32[1024,2048]{1,0:T(8,128)} %fusion.60, f32[1024,2048]{1,0:T(8,128)} %fusion.57, bf16[512,2048]{1,0:T(8,128)(2,1)S(1)} %copy-done.15, bf16[1024,512]{1,0:T(8,128)(2,1)S(1)} %copy-done.81, f32[]{:T(128)} %bitcast.62), kind=kOutput, calls=%fused_computation.6 | convolution fusion | flops 2155347968 | bytes 36700164 | tf_op jit(solution)/shard_map/dot_general | solution.py:48
  731.0 10.3 collective-permute-done.86
  749.0 14.8 %collective-permute-done.67 = bf16[512,1024]{1,0:T(8,128)(2,1)S(1)} collective-permute-done((bf16[512,1024]{1,0:T(8,128)(2,1)S(1)}, bf16[512,1024]{1,0:T(8,128)(2,1)S(1)}, u32[]{:S(2)}, u32[]{:S(2)}) %collective-permute-start.67) | collective-permute-done | bytes 1048608 | tf_op jit(solution)/shard_map/ppermute | solution.py:71
  769.7 16.5 %collective-permute-done.69 = bf16[512,1024]{1,0:T(8,128)(2,1)S(1)} collective-permute-done((bf16[512,1024]{1,0:T(8,128)(2,1)S(1)}, bf16[512,1024]{1,0:T(8,128)(2,1)S(1)}, u32[]{:S(2)}, u32[]{:S(2)}) %collective-permute-start.69) | collective-permute-done | bytes 1048608 | tf_op jit(solution)/shard_map/ppermute | solution.py:71
  788.2 14.1 %collective-permute-done.47 = bf16[256,512]{1,0:T(8,128)(2,1)S(1)} collective-permute-done((bf16[256,512]{1,0:T(8,128)(2,1)S(1)}, bf16[256,512]{1,0:T(8,128)(2,1)S(1)}, u32[]{:S(2)}, u32[]{:S(2)}) %collective-permute-start.47) | collective-permute-done | bytes 262176 | tf_op jit(solution)/shard_map/ppermute | solution.py:71
  837.6 8.8 collective-permute-done.58
  867.5 18.9 %collective-permute-done.91 = bf16[128,2048]{1,0:T(8,128)(2,1)} collective-permute-done((bf16[128,2048]{1,0:T(8,128)(2,1)}, bf16[128,2048]{1,0:T(8,128)(2,1)}, u32[]{:S(2)}, u32[]{:S(2)}) %collective-permute-start.91) | collective-permute-done | bytes 524320 | tf_op jit(solution)/shard_map/ppermute | solution.py:71
  896.3 10.0 collective-permute-done.89
  911.7 15.1 %collective-permute-done.75 = bf16[512,1024]{1,0:T(8,128)(2,1)} collective-permute-done((bf16[512,1024]{1,0:T(8,128)(2,1)}, bf16[512,1024]{1,0:T(8,128)(2,1)}, u32[]{:S(2)}, u32[]{:S(2)}) %collective-permute-start.75) | collective-permute-done | bytes 1048608 | tf_op jit(solution)/shard_map/ppermute | solution.py:71
  931.4 12.0 %collective-permute-done.77 = bf16[512,1024]{1,0:T(8,128)(2,1)S(1)} collective-permute-done((bf16[512,1024]{1,0:T(8,128)(2,1)}, bf16[512,1024]{1,0:T(8,128)(2,1)S(1)}, u32[]{:S(2)}, u32[]{:S(2)}) %collective-permute-start.77) | collective-permute-done | bytes 1048608 | tf_op jit(solution)/shard_map/ppermute | solution.py:71
  961.9 21.2 %collective-permute-done.63 = bf16[256,2048]{1,0:T(8,128)(2,1)} collective-permute-done((bf16[256,2048]{1,0:T(8,128)(2,1)}, bf16[256,2048]{1,0:T(8,128)(2,1)}, u32[]{:S(2)}, u32[]{:S(2)}) %collective-permute-start.63) | collective-permute-done | bytes 1048608 | tf_op jit(solution)/shard_map/ppermute | solution.py:71
  1024.0 40.0 %all-reduce.10.cloned.1.call-done = bf16[256,2048]{1,0:T(8,128)(2,1)} async-done(((bf16[256,2048]{1,0:T(8,128)(2,1)}), bf16[256,2048]{1,0:T(8,128)(2,1)}) %all-reduce.10.cloned.1.call-update) | async-done | bytes 1048592 | tf_op jit(solution)/shard_map/psum | solution.py:496
  (1029 shorter events, 669.2 us)
Async XLA Ops:
  7.2 132.0 %all-gather.8.cloned.1.call-start = ((), (), s32[]{:S(2)}) async-start(), calls=%async_computation.5 | async-start | bytes 2785280 | tf_op jit(solution)/shard_map/all_gather | solution.py:222
  17.5 80.3 %collective-permute-start.3 = (bf16[256,1664]{1,0:T(8,128)(2,1)}, bf16[256,1664]{1,0:T(8,128)(2,1)}, u32[]{:S(2)}, u32[]{:S(2)}) collective-permute-start(bf16[256,1664]{1,0:T(8,128)(2,1)} %pad_maximum_fusion.16), channel_id=1, source_target_pairs={{0,1},{1,0},{2,3},{3,2},{4,5},{5,4},{6,7},{7,6},{8,9},{9,8},{10,11... | collective-permute-start | bytes 2555912 | tf_op jit(solution)/shard_map/ppermute | solution.py:71
  18.0 66.6 %collective-permute-start.8 = (bf16[256,2048]{1,0:T(8,128)(2,1)}, bf16[256,2048]{1,0:T(8,128)(2,1)}, u32[]{:S(2)}, u32[]{:S(2)}) collective-permute-start(bf16[256,2048]{1,0:T(8,128)(2,1)} %param.20), channel_id=1, source_target_pairs={{0,4},{1,5},{2,6},{3,7},{4,0},{5,1},{6,2},{7,3},{8,12},{9,13},{10,... | collective-permute-start | bytes 3145736 | tf_op jit(solution)/shard_map/ppermute | solution.py:71
  84.6 102.7 %collective-permute-start.38 = (bf16[256,1024]{1,0:T(8,128)(2,1)}, bf16[256,1024]{1,0:T(8,128)(2,1)}, u32[]{:S(2)}, u32[]{:S(2)}) collective-permute-start(bf16[256,1024]{1,0:T(8,128)(2,1)} %get-tuple-element.175), channel_id=1, source_target_pairs={{0,1},{1,0},{2,3},{3,2},{4,5},{5,4},{6,7},{7,6},{8,9},{9,8},{10,11... | collective-permute-start | bytes 1572872 | tf_op jit(solution)/shard_map/ppermute | solution.py:71
  104.3 295.5 %collective-permute-start.33 = (bf16[512,1024]{1,0:T(8,128)(2,1)}, bf16[512,1024]{1,0:T(8,128)(2,1)}, u32[]{:S(2)}, u32[]{:S(2)}) collective-permute-start(bf16[512,1024]{1,0:T(8,128)(2,1)} %add_convert_fusion.25), channel_id=1, source_target_pairs={{0,4},{1,5},{2,6},{3,7},{4,0},{5,1},{6,2},{7,3},{8,12},{9,13},{10,... | collective-permute-start | bytes 3145736 | tf_op jit(solution)/shard_map/ppermute | solution.py:71
  114.8 138.6 %collective-permute-start.15 = (bf16[512,1024]{1,0:T(8,128)(2,1)}, bf16[512,1024]{1,0:T(8,128)(2,1)}, u32[]{:S(2)}, u32[]{:S(2)}) collective-permute-start(bf16[512,1024]{1,0:T(8,128)(2,1)} %add_convert_fusion.33), channel_id=1, source_target_pairs={{0,4},{1,5},{2,6},{3,7},{4,0},{5,1},{6,2},{7,3},{8,12},{9,13},{10,... | collective-permute-start | bytes 3145736 | tf_op jit(solution)/shard_map/ppermute | solution.py:71
  134.6 85.0 %collective-permute-start.10 = (bf16[1024,2048]{1,0:T(8,128)(2,1)}, bf16[1024,2048]{1,0:T(8,128)(2,1)}, u32[]{:S(2)}, u32[]{:S(2)}) collective-permute-start(bf16[1024,2048]{1,0:T(8,128)(2,1)} %constant_dynamic-update-slice_fusion.25), channel_id=1, source_target_pairs={{0,1},{1,0},{2,3},{3,2},{4,5},{5,4},{6,7},{7,6},{8,9},{9,8},{10,11... | collective-permute-start | bytes 12582920 | tf_op jit(solution)/shard_map/ppermute | solution.py:71
  178.6 100.2 %all-gather.12.cloned.1.call-start = ((), (), s32[]{:S(2)}) async-start(), calls=%async_computation.7 | async-start | bytes 2621440 | tf_op jit(solution)/shard_map/all_gather | solution.py:281
  181.4 157.5 %all-gather.10.cloned.1.call-start = ((), (), s32[]{:S(2)}) async-start(), calls=%async_computation.6 | async-start | bytes 2621440 | tf_op jit(solution)/shard_map/all_gather | solution.py:345
  229.5 341.0 %reduce-scatter.4.cloned.1.call-start = ((), (), s32[]{:S(2)}) async-start(), calls=%async_computation.8 | async-start | bytes 2785280 | tf_op jit(solution)/shard_map/reduce_scatter | solution.py:403
  298.3 80.5 %collective-permute-start.28 = (bf16[128,2048]{1,0:T(8,128)(2,1)}, bf16[128,2048]{1,0:T(8,128)(2,1)S(1)}, u32[]{:S(2)}, u32[]{:S(2)}) collective-permute-start(bf16[128,2048]{1,0:T(8,128)(2,1)} %get-tuple-element.110), channel_id=1, source_target_pairs={{0,2},{1,3},{2,0},{3,1},{4,6},{5,7},{6,4},{7,5},{8,10},{9,11},{10,... | collective-permute-start | bytes 1572872 | tf_op jit(solution)/shard_map/ppermute | solution.py:71
  378.8 68.2 %collective-permute-start.36 = (bf16[128,2048]{1,0:T(8,128)(2,1)}, bf16[128,2048]{1,0:T(8,128)(2,1)S(1)}, u32[]{:S(2)}, u32[]{:S(2)}) collective-permute-start(bf16[128,2048]{1,0:T(8,128)(2,1)} %get-tuple-element.96), channel_id=1, source_target_pairs={{0,4},{1,5},{2,6},{3,7},{4,0},{5,1},{6,2},{7,3},{8,12},{9,13},{10,... | collective-permute-start | bytes 1572872 | tf_op jit(solution)/shard_map/ppermute | solution.py:71
  388.4 65.9 %collective-permute-start.37 = (bf16[128,2048]{1,0:T(8,128)(2,1)S(1)}, bf16[128,2048]{1,0:T(8,128)(2,1)S(1)}, u32[]{:S(2)}, u32[]{:S(2)}) collective-permute-start(bf16[128,2048]{1,0:T(8,128)(2,1)S(1)} %get-tuple-element.94), channel_id=1, source_target_pairs={{0,4},{1,5},{2,6},{3,7},{4,0},{5,1},{6,2},{7,3},{8,12},{9,13},{10,... | collective-permute-start | bytes 1572872 | tf_op jit(solution)/shard_map/ppermute | solution.py:71
  530.6 147.7 %collective-permute-start.82 = (bf16[128,2048]{1,0:T(8,128)(2,1)}, bf16[128,2048]{1,0:T(8,128)(2,1)}, u32[]{:S(2)}, u32[]{:S(2)}) collective-permute-start(bf16[128,2048]{1,0:T(8,128)(2,1)} %get-tuple-element.141), channel_id=1, source_target_pairs={{0,4},{1,5},{2,6},{3,7},{4,0},{5,1},{6,2},{7,3},{8,12},{9,13},{10,... | collective-permute-start | bytes 1572872 | tf_op jit(solution)/shard_map/ppermute | solution.py:71
  531.3 193.6 %collective-permute-start.81 = (bf16[128,2048]{1,0:T(8,128)(2,1)}, bf16[128,2048]{1,0:T(8,128)(2,1)}, u32[]{:S(2)}, u32[]{:S(2)}) collective-permute-start(bf16[128,2048]{1,0:T(8,128)(2,1)} %get-tuple-element.140), channel_id=1, source_target_pairs={{0,4},{1,5},{2,6},{3,7},{4,0},{5,1},{6,2},{7,3},{8,12},{9,13},{10,... | collective-permute-start | bytes 1572872 | tf_op jit(solution)/shard_map/ppermute | solution.py:71
  536.3 153.9 %collective-permute-start.85 = (bf16[128,2048]{1,0:T(8,128)(2,1)}, bf16[128,2048]{1,0:T(8,128)(2,1)}, u32[]{:S(2)}, u32[]{:S(2)}) collective-permute-start(bf16[128,2048]{1,0:T(8,128)(2,1)} %get-tuple-element.143), channel_id=1, source_target_pairs={{0,2},{1,3},{2,0},{3,1},{4,6},{5,7},{6,4},{7,5},{8,10},{9,11},{10,... | collective-permute-start | bytes 1572872 | tf_op jit(solution)/shard_map/ppermute | solution.py:71
  537.9 192.5 %collective-permute-start.84 = (bf16[128,2048]{1,0:T(8,128)(2,1)}, bf16[128,2048]{1,0:T(8,128)(2,1)}, u32[]{:S(2)}, u32[]{:S(2)}) collective-permute-start(bf16[128,2048]{1,0:T(8,128)(2,1)} %get-tuple-element.142), channel_id=1, source_target_pairs={{0,2},{1,3},{2,0},{3,1},{4,6},{5,7},{6,4},{7,5},{8,10},{9,11},{10,... | collective-permute-start | bytes 1572872 | tf_op jit(solution)/shard_map/ppermute | solution.py:71
  540.7 155.7 %collective-permute-start.66 = (bf16[512,1024]{1,0:T(8,128)(2,1)}, bf16[512,1024]{1,0:T(8,128)(2,1)}, u32[]{:S(2)}, u32[]{:S(2)}) collective-permute-start(bf16[512,1024]{1,0:T(8,128)(2,1)} %convolution_convert_fusion.17), channel_id=1, source_target_pairs={{0,2},{1,3},{2,0},{3,1},{4,6},{5,7},{6,4},{7,5},{8,10},{9,11},{10,... | collective-permute-start | bytes 3145736 | tf_op jit(solution)/shard_map/ppermute | solution.py:71
  596.0 362.8 %reduce-scatter.8.cloned.1.call-start = ((), (), s32[]{:S(2)}) async-start(), calls=%async_computation.10 | async-start | bytes 2621440 | tf_op jit(solution)/shard_map/reduce_scatter | solution.py:516
  662.5 323.4 %all-gather.14.cloned.1.call-start = ((), (), s32[]{:S(2)}) async-start(), calls=%async_computation.12 | async-start | bytes 2949120 | tf_op jit(solution)/shard_map/all_gather | solution.py:545
  748.4 111.5 %collective-permute-start.88 = (bf16[128,2048]{1,0:T(8,128)(2,1)}, bf16[128,2048]{1,0:T(8,128)(2,1)}, u32[]{:S(2)}, u32[]{:S(2)}) collective-permute-start(bf16[128,2048]{1,0:T(8,128)(2,1)} %get-tuple-element.145), channel_id=1, source_target_pairs={{0,4},{1,5},{2,6},{3,7},{4,0},{5,1},{6,2},{7,3},{8,12},{9,13},{10,... | collective-permute-start | bytes 1572872 | tf_op jit(solution)/shard_map/ppermute | solution.py:71
  822.7 176.9 %all-gather.16.cloned.1.call-start = ((), (), s32[]{:S(2)}) async-start(), calls=%async_computation.13 | async-start | bytes 1310720 | tf_op jit(solution)/shard_map/all_gather | solution.py:544
  864.2 157.8 %reduce-scatter.6.cloned.1.call-start = ((), (), s32[]{:S(2)}) async-start(), calls=%async_computation.9 | async-start | bytes 2621440 | tf_op jit(solution)/shard_map/reduce_scatter | solution.py:483
  896.2 167.8 %all-reduce.10.cloned.1.call-start = ((), (), s32[]{:S(2)}) async-start(), calls=%async_computation.11 | async-start | bytes 2097152 | tf_op jit(solution)/shard_map/psum | solution.py:496
  (254 other events, 3832.6 us)
Sparse Core Ops, SparseCore 0:
  19.4 49.5 all-gather.7
  181.5 45.4 all-gather.11
  229.7 46.9 all-gather.9
  524.5 45.9 reduce-scatter.3
  662.6 44.9 reduce-scatter.7
  822.8 50.9 all-gather.13
  875.3 26.7 all-gather.15
  905.0 42.9 reduce-scatter.5
  1011.9 52.0 all-reduce.9
where the time goes:
time: 1080 us; the launch traced here: 1070 us
  waiting for transfers between devices  354 us (33%)
  matrix products  244 us (23%)
  local copies, waits for them, and re-layouts  201 us (19%)
  other arithmetic  161 us (15%)
  starting transfers between devices  84.6 us (8%)
  between operations  28.7 us (3%)
    ppermute x93, waiting for transfers between devices, swap(): return lax.ppermute(values, 'wt', [(i, i ^ bit) for i in range(total)])  300 us
    dot_general x55, matrix products, dot(): lax.dot_general(left, right, (dims, ((), ())), preferred_element_type=F32)  229 us
    unnamed x514, local copies, waits for them, and re-layouts  94.1 us
    ppermute x93, starting transfers between devices, swap(): return lax.ppermute(values, 'wt', [(i, i ^ bit) for i in range(total)])  74.4 us
    psum x1, waiting for transfers between devices, body(): out_grad = lax.psum(out_sum, 'seq')  40 us
    convert_element_type x13, other arithmetic, scatter_chips(): held[mask ^ bit] = total.astype(BF) if rest else total  23.1 us
  transfers between devices with their start and end apart: 104, of which 32 were waited for; matrix products, arithmetic and copies ran while one was open for 50% of the time, Pallas kernels for 0%

commit v1 on v0

--- a/solution.py
+++ b/solution.py
@@ -538,13 +538,13 @@
     ).astype(BF)
     for e in range(3, local_experts):
         start_expert(e, grad_normed_low)
+    grads = [later(g, moe_out) for g in grads]
     value_sum = scatter_rows(hidden, grads[2], 0)
     query_sum = scatter_rows(hidden, grads[0], 1)
     key_sum = scatter_rows(hidden, grads[1], 0)
     collected_value = lax.all_gather(value_sum, "seq", axis=0)
-    collected = lax.all_gather(
-        jnp.concatenate([query_sum, key_sum, small_sum], axis=1), "seq", axis=0
-    )
+    joined = jnp.concatenate([query_sum, key_sum, small_sum], axis=1)
+    collected = lax.all_gather(joined, "seq", axis=0)
     qkv_out = jnp.concatenate(
         [collected[z, :, :part] for z in range(seq_total)]
         + [collected[z, :, part : 2 * part] for z in range(seq_total)]

time: 1080 us -> 1070 us (level)
  local copies, waits for them, and re-layouts: 201 us -> 179 us
  matrix products: 244 us -> 257 us
    ppermute x93, waiting for transfers between devices: 300 us -> 336 us  [swap(): return lax.ppermute(values, 'wt', [(i, i ^ bit) for i in range(total)])]
    psum x1, waiting for transfers between devices: 40 us -> 7.43 us  [body(): out_grad = lax.psum(out_sum, 'seq')]
    unnamed x514 -> x544, local copies, waits for them, and re-layouts: 94.1 us -> 67.4 us
  transfers between devices with their start and end apart: 104 -> 104, of which waited for: 32 -> 33; matrix products, arithmetic and copies ran while one was open for 50% -> 48% of each run, Pallas kernels for 0% -> 0%
where the time goes in v1:
time: 1070 us; the launch traced here: 1060 us
  waiting for transfers between devices  359 us (34%)
  matrix products  257 us (24%)
  local copies, waits for them, and re-layouts  179 us (17%)
  other arithmetic  151 us (14%)
  starting transfers between devices  90.4 us (8%)
  between operations  29.4 us (3%)
    ppermute x93, waiting for transfers between devices, swap(): return lax.ppermute(values, 'wt', [(i, i ^ bit) for i in range(total)])  336 us
    dot_general x55, matrix products, dot(): lax.dot_general(left, right, (dims, ((), ())), preferred_element_type=F32)  239 us
    ppermute x93, starting transfers between devices, swap(): return lax.ppermute(values, 'wt', [(i, i ^ bit) for i in range(total)])  80 us
    unnamed x544, local copies, waits for them, and re-layouts  67.4 us
  transfers between devices with their start and end apart: 104, of which 33 were waited for; matrix products, arithmetic and copies ran while one was open for 48% of the time, Pallas kernels for 0%

profile of v1, /device:TPU:0, one launch (start us, length us, event | category | flops | bytes accessed | tf_op | source)
XLA Modules:
  0.0 1064.8 jit_solution(16892915214961509788)
XLA Ops:
  87.5 9.6 collective-permute-done.2
  117.0 24.1 %collective-permute-done.9 = bf16[256,2048]{1,0:T(8,128)(2,1)S(1)} collective-permute-done((bf16[256,2048]{1,0:T(8,128)(2,1)}, bf16[256,2048]{1,0:T(8,128)(2,1)S(1)}, u32[]{:S(2)}, u32[]{:S(2)}) %collective-permute-start.9) | collective-permute-done | bytes 1048608 | tf_op jit(solution)/shard_map/ppermute | solution.py:71
  152.6 8.6 fusion.235
  205.8 14.9 %collective-permute-done.26 = bf16[512,1024]{1,0:T(8,128)(2,1)} collective-permute-done((bf16[512,1024]{1,0:T(8,128)(2,1)}, bf16[512,1024]{1,0:T(8,128)(2,1)}, u32[]{:S(2)}, u32[]{:S(2)}) %collective-permute-start.26) | collective-permute-done | bytes 1048608 | tf_op jit(solution)/shard_map/ppermute | solution.py:71
  239.8 20.1 %collective-permute-done.18 = bf16[128,2048]{1,0:T(8,128)(2,1)} collective-permute-done((bf16[128,2048]{1,0:T(8,128)(2,1)}, bf16[128,2048]{1,0:T(8,128)(2,1)}, u32[]{:S(2)}, u32[]{:S(2)}) %collective-permute-start.18) | collective-permute-done | bytes 524320 | tf_op jit(solution)/shard_map/ppermute | solution.py:71
  267.8 18.4 %collective-permute-done.16 = bf16[512,1024]{1,0:T(8,128)(2,1)S(1)} collective-permute-done((bf16[512,1024]{1,0:T(8,128)(2,1)}, bf16[512,1024]{1,0:T(8,128)(2,1)S(1)}, u32[]{:S(2)}, u32[]{:S(2)}) %collective-permute-start.16) | collective-permute-done | bytes 1048608 | tf_op jit(solution)/shard_map/ppermute | solution.py:71
  291.3 14.4 %collective-permute-done.23 = bf16[128,2048]{1,0:T(8,128)(2,1)} collective-permute-done((bf16[128,2048]{1,0:T(8,128)(2,1)}, bf16[128,2048]{1,0:T(8,128)(2,1)}, u32[]{:S(2)}, u32[]{:S(2)}) %collective-permute-start.23) | collective-permute-done | bytes 524320 | tf_op jit(solution)/shard_map/ppermute | solution.py:71
  334.7 12.9 %collective-permute-done.32 = bf16[512,1024]{1,0:T(8,128)(2,1)} collective-permute-done((bf16[512,1024]{1,0:T(8,128)(2,1)}, bf16[512,1024]{1,0:T(8,128)(2,1)}, u32[]{:S(2)}, u32[]{:S(2)}) %collective-permute-start.32) | collective-permute-done | bytes 1048608 | tf_op jit(solution)/shard_map/ppermute | solution.py:71
  396.9 9.7 fusion.41
  428.4 10.3 fusion.40
  447.8 10.0 fusion.39
  467.9 18.1 %add_add_fusion.1 = f32[1024,2048]{1,0:T(8,128)} fusion(f32[1024,2048]{1,0:T(8,128)} %fusion.39, f32[1024,2048]{1,0:T(8,128)} %fusion.41, f32[1024,2048]{1,0:T(8,128)} %fusion.40, bf16[1024,512]{1,0:T(8,128)(2,1)} %get-tuple-element.112, bf16[1024,512]{1,0:T(8,128)(2,1)} %get-tuple-element.111, bf16[512,1024]{1,0:T(8,128)(2,1)} %copy-done.27, ...), kind=kOutput, calls=%fused_computation.7 | convolution fusion | flops 4322230272 | bytes 39845888 | tf_op jit(solution)/shard_map/dot_general | solution.py:48
  550.0 14.0 %reduce-scatter.4.cloned.1.call-done = bf16[128,2080]{1,0:T(8,128)(2,1)} async-done(((bf16[512,2080]{1,0:T(8,128)(2,1)}), bf16[128,2080]{1,0:T(8,128)(2,1)}) %reduce-scatter.4.cloned.1.call-update) | async-done | bytes 532496 | tf_op jit(solution)/shard_map/reduce_scatter | solution.py:403
  635.9 11.1 %add_add_fusion = f32[1024,2048]{1,0:T(8,128)S(1)} fusion(f32[1024,2048]{1,0:T(8,128)} %fusion.54, f32[1024,2048]{1,0:T(8,128)} %fusion.60, f32[1024,2048]{1,0:T(8,128)} %fusion.57, bf16[512,2048]{1,0:T(8,128)(2,1)S(1)} %copy-done.17, bf16[1024,512]{1,0:T(8,128)(2,1)} %get-tuple-element.123, f32[]{:T(128)} %bitcast.62), kind=kOutput, calls=%fused_computation.6 | convolution fusion | flops 2155347968 | bytes 36700164 | tf_op jit(solution)/shard_map/dot_general | solution.py:48
  722.1 35.7 %collective-permute-done.55 = bf16[256,128]{1,0:T(8,128)(2,1)S(1)} collective-permute-done((bf16[256,128]{1,0:T(8,128)(2,1)S(1)}, bf16[256,128]{1,0:T(8,128)(2,1)S(1)}, u32[]{:S(2)}, u32[]{:S(2)}) %collective-permute-start.55) | collective-permute-done | bytes 65568 | tf_op jit(solution)/shard_map/ppermute | solution.py:71
  762.9 10.4 collective-permute-done.56
  788.1 22.9 %collective-permute-done.86 = bf16[128,2048]{1,0:T(8,128)(2,1)S(1)} collective-permute-done((bf16[128,2048]{1,0:T(8,128)(2,1)S(1)}, bf16[128,2048]{1,0:T(8,128)(2,1)S(1)}, u32[]{:S(2)}, u32[]{:S(2)}) %collective-permute-start.86) | collective-permute-done | bytes 524320 | tf_op jit(solution)/shard_map/ppermute | solution.py:71
  831.9 15.2 %collective-permute-done.63 = bf16[256,2048]{1,0:T(8,128)(2,1)} collective-permute-done((bf16[256,2048]{1,0:T(8,128)(2,1)}, bf16[256,2048]{1,0:T(8,128)(2,1)}, u32[]{:S(2)}, u32[]{:S(2)}) %collective-permute-start.63) | collective-permute-done | bytes 1048608 | tf_op jit(solution)/shard_map/ppermute | solution.py:71
  856.3 13.2 %collective-permute-done.62 = bf16[256,2048]{1,0:T(8,128)(2,1)} collective-permute-done((bf16[256,2048]{1,0:T(8,128)(2,1)}, bf16[256,2048]{1,0:T(8,128)(2,1)}, u32[]{:S(2)}, u32[]{:S(2)}) %collective-permute-start.62) | collective-permute-done | bytes 1048608 | tf_op jit(solution)/shard_map/ppermute | solution.py:71
  905.9 14.6 %collective-permute-done.59 = bf16[256,512]{1,0:T(8,128)(2,1)S(1)} collective-permute-done((bf16[256,512]{1,0:T(8,128)(2,1)S(1)}, bf16[256,512]{1,0:T(8,128)(2,1)S(1)}, u32[]{:S(2)}, u32[]{:S(2)}) %collective-permute-start.59) | collective-permute-done | bytes 262176 | tf_op jit(solution)/shard_map/ppermute | solution.py:71
  942.9 26.8 %collective-permute-done.91 = bf16[128,2048]{1,0:T(8,128)(2,1)} collective-permute-done((bf16[128,2048]{1,0:T(8,128)(2,1)}, bf16[128,2048]{1,0:T(8,128)(2,1)}, u32[]{:S(2)}, u32[]{:S(2)}) %collective-permute-start.91) | collective-permute-done | bytes 524320 | tf_op jit(solution)/shard_map/ppermute | solution.py:71
  977.4 16.6 %collective-permute-done.89 = bf16[128,2048]{1,0:T(8,128)(2,1)S(1)} collective-permute-done((bf16[128,2048]{1,0:T(8,128)(2,1)S(1)}, bf16[128,2048]{1,0:T(8,128)(2,1)S(1)}, u32[]{:S(2)}, u32[]{:S(2)}) %collective-permute-start.89) | collective-permute-done | bytes 524320 | tf_op jit(solution)/shard_map/ppermute | solution.py:71
  999.7 12.5 %collective-permute-done.75 = bf16[512,1024]{1,0:T(8,128)(2,1)S(1)} collective-permute-done((bf16[512,1024]{1,0:T(8,128)(2,1)S(1)}, bf16[512,1024]{1,0:T(8,128)(2,1)S(1)}, u32[]{:S(2)}, u32[]{:S(2)}) %collective-permute-start.75) | collective-permute-done | bytes 1048608 | tf_op jit(solution)/shard_map/ppermute | solution.py:71
  1016.6 15.7 %collective-permute-done.77 = bf16[512,1024]{1,0:T(8,128)(2,1)S(1)} collective-permute-done((bf16[512,1024]{1,0:T(8,128)(2,1)S(1)}, bf16[512,1024]{1,0:T(8,128)(2,1)S(1)}, u32[]{:S(2)}, u32[]{:S(2)}) %collective-permute-start.77) | collective-permute-done | bytes 1048608 | tf_op jit(solution)/shard_map/ppermute | solution.py:71
  (1060 shorter events, 655.7 us)
Async XLA Ops:
  7.2 141.2 %all-gather.8.cloned.1.call-start = ((), (), s32[]{:S(2)}) async-start(), calls=%async_computation.5 | async-start | bytes 2785280 | tf_op jit(solution)/shard_map/all_gather | solution.py:222
  17.5 80.5 %collective-permute-start.3 = (bf16[256,1664]{1,0:T(8,128)(2,1)}, bf16[256,1664]{1,0:T(8,128)(2,1)}, u32[]{:S(2)}, u32[]{:S(2)}) collective-permute-start(bf16[256,1664]{1,0:T(8,128)(2,1)} %pad_maximum_fusion.16), channel_id=1, source_target_pairs={{0,1},{1,0},{2,3},{3,2},{4,5},{5,4},{6,7},{7,6},{8,9},{9,8},{10,11... | collective-permute-start | bytes 2555912 | tf_op jit(solution)/shard_map/ppermute | solution.py:71
  84.8 111.5 %collective-permute-start.38 = (bf16[256,1024]{1,0:T(8,128)(2,1)}, bf16[256,1024]{1,0:T(8,128)(2,1)}, u32[]{:S(2)}, u32[]{:S(2)}) collective-permute-start(bf16[256,1024]{1,0:T(8,128)(2,1)} %get-tuple-element.175), channel_id=1, source_target_pairs={{0,1},{1,0},{2,3},{3,2},{4,5},{5,4},{6,7},{7,6},{8,9},{9,8},{10,11... | collective-permute-start | bytes 1572872 | tf_op jit(solution)/shard_map/ppermute | solution.py:71
  104.5 268.0 %collective-permute-start.28 = (bf16[128,2048]{1,0:T(8,128)(2,1)}, bf16[128,2048]{1,0:T(8,128)(2,1)}, u32[]{:S(2)}, u32[]{:S(2)}) collective-permute-start(bf16[128,2048]{1,0:T(8,128)(2,1)} %get-tuple-element.110), channel_id=1, source_target_pairs={{0,2},{1,3},{2,0},{3,1},{4,6},{5,7},{6,4},{7,5},{8,10},{9,11},{10,... | collective-permute-start | bytes 1572872 | tf_op jit(solution)/shard_map/ppermute | solution.py:71
  113.7 148.7 %collective-permute-start.15 = (bf16[512,1024]{1,0:T(8,128)(2,1)}, bf16[512,1024]{1,0:T(8,128)(2,1)}, u32[]{:S(2)}, u32[]{:S(2)}) collective-permute-start(bf16[512,1024]{1,0:T(8,128)(2,1)} %add_convert_fusion.33), channel_id=1, source_target_pairs={{0,4},{1,5},{2,6},{3,7},{4,0},{5,1},{6,2},{7,3},{8,12},{9,13},{10,... | collective-permute-start | bytes 3145736 | tf_op jit(solution)/shard_map/ppermute | solution.py:71
  143.8 85.9 %collective-permute-start.10 = (bf16[1024,2048]{1,0:T(8,128)(2,1)}, bf16[1024,2048]{1,0:T(8,128)(2,1)}, u32[]{:S(2)}, u32[]{:S(2)}) collective-permute-start(bf16[1024,2048]{1,0:T(8,128)(2,1)} %constant_dynamic-update-slice_fusion.25), channel_id=1, source_target_pairs={{0,1},{1,0},{2,3},{3,2},{4,5},{5,4},{6,7},{7,6},{8,9},{9,8},{10,11... | collective-permute-start | bytes 12582920 | tf_op jit(solution)/shard_map/ppermute | solution.py:71
  187.5 101.3 %all-gather.12.cloned.1.call-start = ((), (), s32[]{:S(2)}) async-start(), calls=%async_computation.7 | async-start | bytes 2621440 | tf_op jit(solution)/shard_map/all_gather | solution.py:281
  190.3 130.5 %all-gather.10.cloned.1.call-start = ((), (), s32[]{:S(2)}) async-start(), calls=%async_computation.6 | async-start | bytes 2621440 | tf_op jit(solution)/shard_map/all_gather | solution.py:345
  239.6 324.5 %reduce-scatter.4.cloned.1.call-start = ((), (), s32[]{:S(2)}) async-start(), calls=%async_computation.8 | async-start | bytes 2785280 | tf_op jit(solution)/shard_map/reduce_scatter | solution.py:403
  305.7 76.8 %collective-permute-start.29 = (bf16[128,2048]{1,0:T(8,128)(2,1)}, bf16[128,2048]{1,0:T(8,128)(2,1)}, u32[]{:S(2)}, u32[]{:S(2)}) collective-permute-start(bf16[128,2048]{1,0:T(8,128)(2,1)} %get-tuple-element.110), channel_id=1, source_target_pairs={{0,4},{1,5},{2,6},{3,7},{4,0},{5,1},{6,2},{7,3},{8,12},{9,13},{10,... | collective-permute-start | bytes 1572872 | tf_op jit(solution)/shard_map/ppermute | solution.py:71
  308.2 85.8 %collective-permute-start.33 = (bf16[512,1024]{1,0:T(8,128)(2,1)}, bf16[512,1024]{1,0:T(8,128)(2,1)}, u32[]{:S(2)}, u32[]{:S(2)}) collective-permute-start(bf16[512,1024]{1,0:T(8,128)(2,1)} %add_convert_fusion.25), channel_id=1, source_target_pairs={{0,4},{1,5},{2,6},{3,7},{4,0},{5,1},{6,2},{7,3},{8,12},{9,13},{10,... | collective-permute-start | bytes 3145736 | tf_op jit(solution)/shard_map/ppermute | solution.py:71
  372.5 67.8 %collective-permute-start.36 = (bf16[128,2048]{1,0:T(8,128)(2,1)S(1)}, bf16[128,2048]{1,0:T(8,128)(2,1)S(1)}, u32[]{:S(2)}, u32[]{:S(2)}) collective-permute-start(bf16[128,2048]{1,0:T(8,128)(2,1)S(1)} %copy-done.143), channel_id=1, source_target_pairs={{0,4},{1,5},{2,6},{3,7},{4,0},{5,1},{6,2},{7,3},{8,12},{9,13},{10,... | collective-permute-start | bytes 1572872 | tf_op jit(solution)/shard_map/ppermute | solution.py:71
  523.7 193.3 %collective-permute-start.82 = (bf16[128,2048]{1,0:T(8,128)(2,1)}, bf16[128,2048]{1,0:T(8,128)(2,1)}, u32[]{:S(2)}, u32[]{:S(2)}) collective-permute-start(bf16[128,2048]{1,0:T(8,128)(2,1)} %get-tuple-element.141), channel_id=1, source_target_pairs={{0,4},{1,5},{2,6},{3,7},{4,0},{5,1},{6,2},{7,3},{8,12},{9,13},{10,... | collective-permute-start | bytes 1572872 | tf_op jit(solution)/shard_map/ppermute | solution.py:71
  524.2 249.4 %collective-permute-start.81 = (bf16[128,2048]{1,0:T(8,128)(2,1)}, bf16[128,2048]{1,0:T(8,128)(2,1)}, u32[]{:S(2)}, u32[]{:S(2)}) collective-permute-start(bf16[128,2048]{1,0:T(8,128)(2,1)} %get-tuple-element.140), channel_id=1, source_target_pairs={{0,4},{1,5},{2,6},{3,7},{4,0},{5,1},{6,2},{7,3},{8,12},{9,13},{10,... | collective-permute-start | bytes 1572872 | tf_op jit(solution)/shard_map/ppermute | solution.py:71
  529.4 190.3 %collective-permute-start.85 = (bf16[128,2048]{1,0:T(8,128)(2,1)}, bf16[128,2048]{1,0:T(8,128)(2,1)}, u32[]{:S(2)}, u32[]{:S(2)}) collective-permute-start(bf16[128,2048]{1,0:T(8,128)(2,1)} %get-tuple-element.143), channel_id=1, source_target_pairs={{0,2},{1,3},{2,0},{3,1},{4,6},{5,7},{6,4},{7,5},{8,10},{9,11},{10,... | collective-permute-start | bytes 1572872 | tf_op jit(solution)/shard_map/ppermute | solution.py:71
  533.2 241.2 %collective-permute-start.65 = (bf16[512,1024]{1,0:T(8,128)(2,1)}, bf16[512,1024]{1,0:T(8,128)(2,1)}, u32[]{:S(2)}, u32[]{:S(2)}) collective-permute-start(bf16[512,1024]{1,0:T(8,128)(2,1)} %convolution_convert_fusion.19), channel_id=1, source_target_pairs={{0,2},{1,3},{2,0},{3,1},{4,6},{5,7},{6,4},{7,5},{8,10},{9,11},{10,... | collective-permute-start | bytes 3145736 | tf_op jit(solution)/shard_map/ppermute | solution.py:71
  589.6 231.8 %reduce-scatter.6.cloned.1.call-start = ((), (), s32[]{:S(2)}) async-start(), calls=%async_computation.9 | async-start | bytes 2621440 | tf_op jit(solution)/shard_map/reduce_scatter | solution.py:483
  675.0 153.1 %reduce-scatter.8.cloned.1.call-start = ((), (), s32[]{:S(2)}) async-start(), calls=%async_computation.10 | async-start | bytes 2621440 | tf_op jit(solution)/shard_map/reduce_scatter | solution.py:516
  702.0 228.3 %all-reduce.10.cloned.1.call-start = ((), (), s32[]{:S(2)}) async-start(), calls=%async_computation.11 | async-start | bytes 2097152 | tf_op jit(solution)/shard_map/psum | solution.py:496
  779.7 160.4 %collective-permute-start.88 = (bf16[128,2048]{1,0:T(8,128)(2,1)}, bf16[128,2048]{1,0:T(8,128)(2,1)}, u32[]{:S(2)}, u32[]{:S(2)}) collective-permute-start(bf16[128,2048]{1,0:T(8,128)(2,1)} %get-tuple-element.145), channel_id=1, source_target_pairs={{0,4},{1,5},{2,6},{3,7},{4,0},{5,1},{6,2},{7,3},{8,12},{9,13},{10,... | collective-permute-start | bytes 1572872 | tf_op jit(solution)/shard_map/ppermute | solution.py:71
  877.6 162.0 %all-gather.14.cloned.1.call-start = ((), (), s32[]{:S(2)}) async-start(), calls=%async_computation.12 | async-start | bytes 2949120 | tf_op jit(solution)/shard_map/all_gather | solution.py:547
  887.1 87.8 %collective-permute-start.87 = (bf16[128,2048]{1,0:T(8,128)(2,1)}, bf16[128,2048]{1,0:T(8,128)(2,1)}, u32[]{:S(2)}, u32[]{:S(2)}) collective-permute-start(bf16[128,2048]{1,0:T(8,128)(2,1)} %get-tuple-element.144), channel_id=1, source_target_pairs={{0,4},{1,5},{2,6},{3,7},{4,0},{5,1},{6,2},{7,3},{8,12},{9,13},{10,... | collective-permute-start | bytes 1572872 | tf_op jit(solution)/shard_map/ppermute | solution.py:71
  890.4 109.2 %collective-permute-start.73 = (bf16[512,1024]{1,0:T(8,128)(2,1)}, bf16[512,1024]{1,0:T(8,128)(2,1)}, u32[]{:S(2)}, u32[]{:S(2)}) collective-permute-start(bf16[512,1024]{1,0:T(8,128)(2,1)} %convolution_convert_fusion.11), channel_id=1, source_target_pairs={{0,2},{1,3},{2,0},{3,1},{4,6},{5,7},{6,4},{7,5},{8,10},{9,11},{10,... | collective-permute-start | bytes 3145736 | tf_op jit(solution)/shard_map/ppermute | solution.py:71
  895.9 154.0 %all-gather.16.cloned.1.call-start = ((), (), s32[]{:S(2)}) async-start(), calls=%async_computation.13 | async-start | bytes 1310720 | tf_op jit(solution)/shard_map/all_gather | solution.py:545
  (269 other events, 3974.1 us)
Sparse Core Ops, SparseCore 0:
  19.4 49.5 all-gather.7
  190.4 46.1 all-gather.11
  239.7 45.8 all-gather.9
  517.6 46.4 reduce-scatter.3
  675.1 44.0 reduce-scatter.5
  722.0 42.8 reduce-scatter.7
  877.7 52.6 all-reduce.9
  931.9 49.2 all-gather.13
  983.3 26.7 all-gather.15
